TPU v7x, 32 devices: a whole 2x2x4 slice. The times are simulated.
32 devices in a mesh: seq: 8 (over y, x, core), tensor: 4 (over z).
Axes of the slice: x: 2, y: 2, z: 4, core: 2. Of those that a mesh axis runs over, the one named last changes fastest.
Arguments:
- tokens: bfloat16 [4096, 8192], P('seq', 'tensor'), may hold values from -6 to 6
- positions: int32 [4096], P('seq'), may hold values from 0 to 4095, each once
- norm_gain: float32 [8192], replicated, may hold values from 0.1 to 1.9
- w_query: bfloat16 [8192, 4096], P('seq', 'tensor'), may hold values from -0.0625 to 0.0625
- w_key: bfloat16 [8192, 1024], P('seq', 'tensor'), may hold values from -0.0625 to 0.0625
- w_value: bfloat16 [8192, 1024], P('seq', 'tensor'), may hold values from -0.0625 to 0.0625
- b_query: float32 [4096], P('tensor'), may hold values from -40 to 40
- b_key: float32 [1024], P('tensor'), may hold values from -40 to 40
- b_value: float32 [1024], P('tensor'), may hold values from -6 to 6
- w_out: bfloat16 [4096, 8192], P('tensor', 'seq'), may hold values from -0.09375 to 0.09375
Outputs:
- mixed: bfloat16 [4096, 8192], P('seq', 'tensor')
- context: bfloat16 [4096, 4096], P('seq', 'tensor')
Inputs may be any that keep to these rules, and one draw needn't show every extreme that they name: positions holds every position 0 to 4095 once.
All inputs are finite; a program needn't handle non-finite values.
Results may differ from a plain program's by a relative error of at most 0.025.
Values may be sent and summed in bfloat16 or wider, within the bound.
A program may use at most 128 MiB of HBM per device.

v0:
```python
import math
import jax
import jax.numpy as jnp
from jax import lax
from jax.sharding import PartitionSpec as P

HD = 128
NORM_EPS = 1e-06
ROPE_BASE = 1000000.0
NEG_FILL = -1e30


def rotate(values_in, positions):
    half_dim = HD // 2
    inv_freq = ROPE_BASE ** (-jnp.arange(half_dim, dtype=jnp.float32) * 2.0 / HD)
    angles = positions.astype(jnp.float32)[:, None] * inv_freq[None, :]
    cosine = jnp.cos(angles)[:, None, :]
    sines = jnp.sin(angles)[:, None, :]
    lower_half = values_in[..., :half_dim]
    upper_half = values_in[..., half_dim:]
    return jnp.concatenate(
        [lower_half * cosine - upper_half * sines, upper_half * cosine + lower_half * sines], -1
    )


def shards(tokens, positions, norm_gain, w_query, w_key, w_value, b_query, b_key, b_value, w_out):
    tok_rows = tokens.shape[0]
    features = lax.all_gather(tokens, "tensor", axis=1, tiled=True)
    inputs = features.astype(jnp.float32)
    inverse_rms = lax.rsqrt(jnp.mean(inputs * inputs, -1, keepdims=True) + NORM_EPS)
    normed = (inputs * inverse_rms * norm_gain[None, :]).astype(jnp.bfloat16)
    w_cat = jnp.concatenate((w_query, w_key, w_value), 1)
    b_cat = jnp.concatenate((b_query, b_key, b_value))
    projected = jnp.dot(
        normed, lax.all_gather(w_cat, "seq", axis=0, tiled=True), preferred_element_type=jnp.float32
    )
    projected = projected + b_cat[None, :]
    query_cols = w_query.shape[1]
    key_cols = w_key.shape[1]
    heads_here = query_cols // HD
    kv_here = key_cols // HD
    group = heads_here // kv_here
    queries = rotate(projected[:, :query_cols].reshape(tok_rows, heads_here, HD), positions).astype(
        jnp.bfloat16
    )
    queries = queries.reshape(tok_rows, kv_here, group, HD)
    keys_rot = rotate(
        projected[:, query_cols : query_cols + key_cols].reshape(tok_rows, kv_here, HD), positions
    ).astype(jnp.bfloat16)
    values = (
        projected[:, query_cols + key_cols :].astype(jnp.bfloat16).reshape(tok_rows, kv_here, HD)
    )
    scale = HD ** (-0.5)

    def attend_block(running, key_block):
        running_max, denominator, numerator = running
        block_keys, block_values, key_pos = key_block
        scores = (
            jnp.einsum("tgcd,sgd->gcts", queries, block_keys, preferred_element_type=jnp.float32)
            * scale
        )
        allowed = (key_pos[None, :] <= positions[:, None])[None, None, :, :]
        scores = jnp.where(allowed, scores, NEG_FILL)
        new_max = jnp.maximum(running_max, jnp.max(scores, -1))
        weights = jnp.where(allowed, jnp.exp(scores - new_max[..., None]), 0.0)
        rescale = jnp.exp(running_max - new_max)
        denominator = denominator * rescale + jnp.sum(weights, -1)
        numerator = numerator * rescale[..., None] + jnp.einsum(
            "gcts,sgd->gctd",
            weights.astype(jnp.bfloat16),
            block_values,
            preferred_element_type=jnp.float32,
        )
        return (new_max, denominator, numerator)

    start_state = (
        jnp.full((kv_here, group, tok_rows), NEG_FILL, jnp.float32),
        jnp.zeros((kv_here, group, tok_rows), jnp.float32),
        jnp.zeros((kv_here, group, tok_rows, HD), jnp.float32),
    )
    all_keys_in = lax.all_gather(keys_rot, "seq", axis=0, tiled=True)
    all_values_in = lax.all_gather(values, "seq", axis=0, tiled=True)
    key_pos = lax.all_gather(positions, "seq", axis=0, tiled=True)
    count = all_keys_in.shape[0]
    width = math.gcd(count, 2048)
    stacked = (
        all_keys_in.reshape(count // width, width, kv_here, HD),
        all_values_in.reshape(count // width, width, kv_here, HD),
        key_pos.reshape(count // width, width),
    )

    def stepper(carried, key_block):
        return (attend_block(carried, key_block), None)

    result, unused = lax.scan(stepper, start_state, stacked)
    unused_max, denominator, numerator = result
    per_head = numerator / denominator[..., None]
    context = (
        jnp.transpose(per_head, (2, 0, 1, 3))
        .reshape(tok_rows, heads_here * HD)
        .astype(jnp.bfloat16)
    )
    out_terms = jnp.dot(
        context,
        lax.all_gather(w_out, "seq", axis=1, tiled=True),
        preferred_element_type=jnp.float32,
    )
    summed = lax.psum_scatter(
        out_terms.astype(jnp.bfloat16), "tensor", scatter_dimension=1, tiled=True
    ).astype(jnp.float32)
    mixed = (tokens.astype(jnp.float32) + summed).astype(jnp.bfloat16)
    return (mixed, context)


def solution(mesh):
    in_specs = (
        P("seq", "tensor"),
        P("seq"),
        P(),
        P("seq", "tensor"),
        P("seq", "tensor"),
        P("seq", "tensor"),
        P("tensor"),
        P("tensor"),
        P("tensor"),
        P("tensor", "seq"),
    )
    out_specs = (P("seq", "tensor"), P("seq", "tensor"))
    return jax.shard_map(shards, mesh=mesh, in_specs=in_specs, out_specs=out_specs, check_vma=False)
```

profile of v0, /device:TPU:0, one launch (start us, length us, event | category | flops | bytes accessed | tf_op | source)
XLA Modules:
  0.0 640.7 jit_solution(5669417840117130354)
XLA Ops:
  8.0 3.1 pad_maximum_fusion
  11.3 1.8 multiply_cosine_fusion
  13.1 148.9 %all-gather.7.cloned.1.call-done = bf16[512,8192]{1,0:T(8,128)(2,1)} async-done(((bf16[512,2048]{1,0:T(8,128)(2,1)}), bf16[512,8192]{1,0:T(8,128)(2,1)}) %all-gather.7.cloned.1.call-update) | async-done | bytes 8388624 | tf_op jit(solution)/shard_map/all_gather | solution.py:28
  161.9 5.1 fusion.20
  167.0 120.2 %all-gather.9.cloned.1.call-done = bf16[8192,1536]{1,0:T(8,128)(2,1)} async-done(((bf16[1024,1536]{1,0:T(8,128)(2,1)}), bf16[8192,1536]{1,0:T(8,128)(2,1)}) %all-gather.9.cloned.1.call-update) | async-done | bytes 25165840 | tf_op jit(solution)/shard_map/all_gather | solution.py:35
  287.2 19.5 %fusion.27 = f32[512,1536]{1,0:T(8,128)S(1)} fusion(bf16[8192,1536]{1,0:T(8,128)(2,1)} %all-gather.9.cloned.1.call-done, bf16[512,8192]{1,0:T(8,128)(2,1)} %all-gather.7.cloned.1.call-done, f32[8192]{0:T(1024)S(1)} %copy-done.10, f32[512]{0:T(512)S(1)} %add_rsqrt_fusion, f32[1536]{0:T(1024)S(1)} %pad_maximum_fusion.3), kind=kOutput, calls=%fused_computation.35 | convolution fusion | flops 12902465536 | bytes 36741120 | tf_op jit(solution)/shard_map/dot_general | solution.py:34
  306.7 1.6 copy-done.1
  309.3 1.2 subtract_convert_fusion.1
  310.6 0.8 pad_maximum_fusion.2
  311.5 1.8 copy_bitcast_fusion
  313.9 8.9 %all-gather = s32[8,1,512]{2,1,0:T(1,128)S(1)} all-gather(s32[1,1,512]{2,1,0:T(1,128)S(1)} %bitcast.69), channel_id=1, replica_groups=mesh['seq'=8,'tensor'=4] {'seq'}, dimensions={0}, use_global_device_ids=true | all-gather | bytes 18432 | tf_op jit(solution)/shard_map/all_gather | solution.py:83
  325.0 1.5 pad_maximum_fusion.1
  326.5 12.8 %all-gather.11.cloned.1.call-done = bf16[4096,2,128]{2,0,1:T(8,128)(2,1)} async-done(((bf16[512,2,128]{2,0,1:T(8,128)(2,1)}), bf16[4096,2,128]{2,0,1:T(8,128)(2,1)}) %all-gather.11.cloned.1.call-update) | async-done | bytes 2097168 | tf_op jit(solution)/shard_map/all_gather | solution.py:81
  339.3 29.6 %all-gather.13.cloned.1.call-done = bf16[4096,2,128]{2,0,1:T(8,128)(2,1)} async-done(((bf16[512,2,128]{2,0,1:T(8,128)(2,1)}), bf16[4096,2,128]{2,0,1:T(8,128)(2,1)}) %all-gather.13.cloned.1.call-update) | async-done | bytes 2097168 | tf_op jit(solution)/shard_map/all_gather | solution.py:82
  368.9 97.0 %while.15 = (s32[]{:T(128)}, f32[2,4,512]{2,1,0:T(4,128)S(1)}, f32[2,4,512]{2,1,0:T(4,128)S(1)}, f32[2,4,512,128]{3,2,1,0:T(8,128)S(1)}, s32[2,2048]{1,0:T(2,128...) while((s32[]{:T(128)}, f32[2,4,512]{2,1,0:T(4,128)S(1)}, ...), condition=%wide.region_4.5_spmd.clone, body=%wide.region_1.4_spmd.clone.sunk | while | flops 4406661120 | bytes 112487544 | solution.py:95
  369.7 16.7 %fusion.48 = (f32[2,4,512]{2,1,0:T(4,128)S(1)}, f32[2,2048,512,4]{2,1,3,0:T(8,128)}) fusion(pred[512,2048]{0,1:T(8,128)(4,1)S(1)} %broadcast_compare_fusion.2, bf16[512,2,4,128]{3,0,2,1:T(8,128)(2,1)} %get-tuple-element.222, bf16[2,2048,2,128]{3,1,0,2:T(8,128)(2,1)} %get-tuple-element.221, s32[]{:T(128)} %get-tuple-element.204), kind=kOutput, calls=%fused_computation.2.clone.1 | convolution fusion | flops 2172645376 | bytes 36717056 | tf_op jit(solution)/shard_map/while/body/eval_jaxpr/tgcd,sgd->gcts/dot_general | solution.py:59
  386.4 14.9 %fusion.49 = f32[2,4,512]{2,1,0:T(4,128)S(1)} fusion(f32[2,2048,512,4]{2,1,3,0:T(8,128)} %get-tuple-element.190, f32[2,4,512]{2,1,0:T(4,128)S(1)} %select_maximum_fusion.2, pred[512,2048]{0,1:T(8,128)(4,1)S(1)} %broadcast_compare_fusion.2), kind=kLoop, calls=%fused_computation.4.clone.1 | loop fusion | flops 41938944 | bytes 34635776 | tf_op jit(solution)/shard_map/while/body/eval_jaxpr/reduce_sum | solution.py:67
  401.3 17.8 %fusion.51 = f32[2,4,512,128]{3,2,1,0:T(8,128)S(1)} fusion(f32[2,4,512,128]{3,2,1,0:T(8,128)S(1)} %get-tuple-element.207, f32[2,2048,512,4]{2,1,3,0:T(8,128)} %get-tuple-element.190, f32[2,4,512]{2,1,0:T(4,128)S(1)} %select_maximum_fusion.2, pred[512,2048]{0,1:T(8,128)(4,1)S(1)} %broadcast_compare_fusion.2, ...), kind=kOutput, calls=%fused_computation.8.clone.1 | convolution fusion | flops 2190999552 | bytes 39879168 | tf_op jit(solution)/shard_map/while/body/eval_jaxpr/gcts,sgd->gctd/dot_general | solution.py:68
  420.0 15.0 %fusion.48 = (f32[2,4,512]{2,1,0:T(4,128)S(1)}, f32[2,2048,512,4]{2,1,3,0:T(8,128)}) fusion(pred[512,2048]{0,1:T(8,128)(4,1)S(1)} %broadcast_compare_fusion.2, bf16[512,2,4,128]{3,0,2,1:T(8,128)(2,1)} %get-tuple-element.222, bf16[2,2048,2,128]{3,1,0,2:T(8,128)(2,1)} %get-tuple-element.221, s32[]{:T(128)} %get-tuple-element.204), kind=kOutput, calls=%fused_computation.2.clone.1 | convolution fusion | flops 2172645376 | bytes 36717056 | tf_op jit(solution)/shard_map/while/body/eval_jaxpr/tgcd,sgd->gcts/dot_general | solution.py:59
  435.0 15.4 %fusion.49 = f32[2,4,512]{2,1,0:T(4,128)S(1)} fusion(f32[2,2048,512,4]{2,1,3,0:T(8,128)} %get-tuple-element.190, f32[2,4,512]{2,1,0:T(4,128)S(1)} %select_maximum_fusion.2, pred[512,2048]{0,1:T(8,128)(4,1)S(1)} %broadcast_compare_fusion.2), kind=kLoop, calls=%fused_computation.4.clone.1 | loop fusion | flops 41938944 | bytes 34635776 | tf_op jit(solution)/shard_map/while/body/eval_jaxpr/reduce_sum | solution.py:67
  450.4 15.5 %fusion.51 = f32[2,4,512,128]{3,2,1,0:T(8,128)S(1)} fusion(f32[2,4,512,128]{3,2,1,0:T(8,128)S(1)} %get-tuple-element.207, f32[2,2048,512,4]{2,1,3,0:T(8,128)} %get-tuple-element.190, f32[2,4,512]{2,1,0:T(4,128)S(1)} %select_maximum_fusion.2, pred[512,2048]{0,1:T(8,128)(4,1)S(1)} %broadcast_compare_fusion.2, ...), kind=kOutput, calls=%fused_computation.8.clone.1 | convolution fusion | flops 2190999552 | bytes 39879168 | tf_op jit(solution)/shard_map/while/body/eval_jaxpr/gcts,sgd->gctd/dot_general | solution.py:68
  468.3 17.2 %convolution_convert_fusion = bf16[512,8192]{1,0:T(8,128)(2,1)} fusion(bf16[512,1024]{1,0:T(8,128)(2,1)S(1)} %convert_element_type.44, bf16[1024,8192]{1,0:T(8,128)(2,1)} %all-gather.15.cloned.1.call-done), kind=kOutput, calls=%fused_computation.30 | convolution fusion | flops 8594128896 | bytes 26214400 | tf_op jit(solution)/shard_map/dot_general | solution.py:103
  485.5 144.7 %reduce-scatter.2.cloned.1.call-done = bf16[512,2048]{1,0:T(8,128)(2,1)} async-done(((bf16[512,8192]{1,0:T(8,128)(2,1)}), bf16[512,2048]{1,0:T(8,128)(2,1)}) %reduce-scatter.2.cloned.1.call-update) | async-done | bytes 2097168 | tf_op jit(solution)/shard_map/reduce_scatter | solution.py:108
  630.2 3.7 add_convert_fusion
  (64 shorter events, 8.6 us)
Async XLA Ops:
  7.2 154.7 %all-gather.7.cloned.1.call-start = ((), (), s32[]{:S(2)}) async-start(), calls=%async_computation.1 | async-start | bytes 10485760 | tf_op jit(solution)/shard_map/all_gather | solution.py:28
  7.9 3.3 copy-start.6
  7.9 3.3 copy-start.7
  7.9 3.3 copy-start.8
  7.9 3.3 copy-start.9
  7.9 279.3 %all-gather.9.cloned.1.call-start = ((), (), s32[]{:S(2)}) async-start(), calls=%async_computation.2 | async-start | bytes 28311552 | tf_op jit(solution)/shard_map/all_gather | solution.py:35
  11.2 328.2 %all-gather.11.cloned.1.call-start = ((), (), s32[]{:S(2)}) async-start(), calls=%async_computation.3 | async-start | bytes 2359296 | tf_op jit(solution)/shard_map/all_gather | solution.py:81
  13.1 274.2 %copy-start.10 = (f32[8192]{0:T(1024)S(1)}, f32[8192]{0:T(1024)}, u32[]{:S(2)}) copy-start(f32[8192]{0:T(1024)} %param.14) | copy-start | bytes 98308
  306.7 1.7 copy-start.1
  309.3 13.6 %copy-start.2 = (f32[512,1536]{1,0:T(8,128)S(1)}, f32[512,1536]{1,0:T(8,128)}, u32[]{:S(2)}) copy-start(f32[512,1536]{1,0:T(8,128)} %copy-done.1) | copy-start | bytes 9437188
  311.4 57.5 %all-gather.13.cloned.1.call-start = ((), (), s32[]{:S(2)}) async-start(), calls=%async_computation.4 | async-start | bytes 2359296 | tf_op jit(solution)/shard_map/all_gather | solution.py:82
  313.3 155.0 %all-gather.15.cloned.1.call-start = ((), (), s32[]{:S(2)}) async-start(), calls=%async_computation.5 | async-start | bytes 18874368 | tf_op jit(solution)/shard_map/all_gather | solution.py:105
  313.9 316.3 %reduce-scatter.2.cloned.1.call-start = ((), (), s32[]{:S(2)}) async-start(), calls=%async_computation.6 | async-start | bytes 10485760 | tf_op jit(solution)/shard_map/reduce_scatter | solution.py:108
  322.9 1.0 copy-start.3
  324.7 44.3 %copy-start.4 = (f32[2,4,512,128]{3,2,1,0:T(8,128)S(1)}, f32[2,4,512,128]{3,2,1,0:T(8,128)}, u32[]{:S(2)}) copy-start(f32[2,4,512,128]{3,2,1,0:T(8,128)} %custom-call.2) | copy-start | bytes 6291460
  468.2 17.2 %copy-start.5 = (bf16[512,1024]{1,0:T(8,128)(2,1)}, bf16[512,1024]{1,0:T(8,128)(2,1)S(1)}, u32[]{:S(2)}) copy-start(bf16[512,1024]{1,0:T(8,128)(2,1)S(1)} %convert_element_type.44) | copy-start | bytes 3145732
  485.4 144.7 %copy-start = (bf16[512,2048]{1,0:T(8,128)(2,1)S(1)}, bf16[512,2048]{1,0:T(8,128)(2,1)}, u32[]{:S(2)}) copy-start(bf16[512,2048]{1,0:T(8,128)(2,1)} %param.12) | copy-start | bytes 6291460
Sparse Core Ops, SparseCore 0:
  9.5 152.3 all-gather.6
  163.8 123.3 all-gather.8
  311.5 27.7 all-gather.10
  341.1 27.7 all-gather.12
  370.7 89.7 all-gather.14
  485.6 144.5 reduce-scatter.1
where the time goes:
time: 641 us
  waiting for transfers between devices  457 us (71%)
  matrix products  102 us (16%)
  other arithmetic  50.8 us (8%)
  between operations  14.4 us (2%)
  blocking collectives  8.87 us (1%)
  local copies, waits for them, and re-layouts  7.19 us (1%)
    all_gather x1, waiting for transfers between devices, shards(): features = lax.all_gather(tokens, 'tensor', axis=1, tiled=True)  149 us
    reduce_scatter x1, waiting for transfers between devices, shards(): lax.psum_scatter(out_terms.astype(jnp.bfloat16), 'tensor', scatter_dimens...  145 us
    all_gather x1, waiting for transfers between devices, shards(): lax.all_gather(w_cat, 'seq', axis=0, tiled=True)  120 us
    dot_general x2, matrix products, attend_block(): jnp.einsum('gcts,sgd->gctd', weights.astype(jnp.bfloat16), block_values,...  33.3 us
    dot_general x2, matrix products, attend_block(): jnp.einsum('tgcd,sgd->gcts', queries, block_keys, preferred_element_type=...  31.7 us
    reduce_sum x2, other arithmetic, attend_block(): denominator = denominator * rescale + jnp.sum(weights, -1)  30.2 us
    all_gather x1, waiting for transfers between devices, shards(): all_values_in = lax.all_gather(values, 'seq', axis=0, tiled=True)  29.6 us
    dot_general x1, matrix products, shards(): jnp.dot(normed, lax.all_gather(w_cat, 'seq', axis=0, tiled=True), preferr...  19.5 us
  transfers between devices with their start and end apart: 6, of which 5 were waited for; matrix products, arithmetic and copies ran while one was open for 18% of the time, Pallas kernels for 0%

commit v1 on v0

--- a/solution.py
+++ b/solution.py
@@ -25,7 +25,12 @@
 
 def shards(tokens, positions, norm_gain, w_query, w_key, w_value, b_query, b_key, b_value, w_out):
     tok_rows = tokens.shape[0]
-    features = lax.all_gather(tokens, "tensor", axis=1, tiled=True)
+    features = jnp.concatenate(
+        jax.lax.all_to_all(
+            jnp.stack(jax.lax.axis_size("tensor") * [tokens], axis=0), "tensor", 0, 0
+        ),
+        axis=1,
+    )
     inputs = features.astype(jnp.float32)
     inverse_rms = lax.rsqrt(jnp.mean(inputs * inputs, -1, keepdims=True) + NORM_EPS)
     normed = (inputs * inverse_rms * norm_gain[None, :]).astype(jnp.bfloat16)

time: 641 us -> 576 us (0.90)
  waiting for transfers between devices: 457 us -> 370 us
  local copies, waits for them, and re-layouts: 7.19 us -> 15.2 us
  other arithmetic: 50.8 us -> 58.8 us
  starting transfers between devices: 0.24 us -> 6.65 us
    all_to_all x0 -> x1, waiting for transfers between devices: none -> 183 us  [shards(): jax.lax.all_to_all(jnp.stack(jax.lax.axis_size('tensor') * [tokens], axis...]
    all_gather x1 -> x0, waiting for transfers between devices: 149 us -> none  [shards(): features = lax.all_gather(tokens, 'tensor', axis=1, tiled=True)]
    all_gather x1, waiting for transfers between devices: 120 us -> 0.01 us  [shards(): lax.all_gather(w_cat, 'seq', axis=0, tiled=True)]
    convert_element_type x0 -> x1, other arithmetic: none -> 7.75 us  [shards(): normed = (inputs * inverse_rms * norm_gain[None, :]).astype(jnp.bfloat16)]
    all_to_all x0 -> x1, starting transfers between devices: none -> 6.49 us  [shards(): jax.lax.all_to_all(jnp.stack(jax.lax.axis_size('tensor') * [tokens], axis...]
  transfers between devices with their start and end apart: 6 -> 6, of which waited for: 5 -> 4; matrix products, arithmetic and copies ran while one was open for 18% -> 22% of each run, Pallas kernels for 0% -> 0%
where the time goes in v1:
time: 576 us; the launch traced here: 575 us
  waiting for transfers between devices  370 us (64%)
  matrix products  102 us (18%)
  other arithmetic  58.8 us (10%)
  local copies, waits for them, and re-layouts  15.2 us (3%)
  between operations  14 us (2%)
  blocking collectives  8.99 us (2%)
  starting transfers between devices  6.65 us (1%)
    all_to_all x1, waiting for transfers between devices, shards(): jax.lax.all_to_all(jnp.stack(jax.lax.axis_size('tensor') * [tokens], axis...  183 us
    reduce_scatter x1, waiting for transfers between devices, shards(): lax.psum_scatter(out_terms.astype(jnp.bfloat16), 'tensor', scatter_dimens...  145 us
    dot_general x2, matrix products, attend_block(): jnp.einsum('gcts,sgd->gctd', weights.astype(jnp.bfloat16), block_values,...  33.3 us
    dot_general x2, matrix products, attend_block(): jnp.einsum('tgcd,sgd->gcts', queries, block_keys, preferred_element_type=...  31.7 us
    reduce_sum x2, other arithmetic, attend_block(): denominator = denominator * rescale + jnp.sum(weights, -1)  30.2 us
    all_gather x1, waiting for transfers between devices, shards(): all_values_in = lax.all_gather(values, 'seq', axis=0, tiled=True)  29.7 us
    dot_general x1, matrix products, shards(): jnp.dot(normed, lax.all_gather(w_cat, 'seq', axis=0, tiled=True), preferr...  19.4 us
    dot_general x1, matrix products, shards(): jnp.dot(context, lax.all_gather(w_out, 'seq', axis=1, tiled=True), prefer...  17.2 us
  transfers between devices with their start and end apart: 6, of which 4 were waited for; matrix products, arithmetic and copies ran while one was open for 22% of the time, Pallas kernels for 0%

profile of v1, /device:TPU:0, one launch (start us, length us, event | category | flops | bytes accessed | tf_op | source)
XLA Modules:
  0.0 574.9 jit_solution(1494898244702085182)
XLA Ops:
  7.2 3.3 pad_maximum_fusion
  10.6 2.5 copy.27
  13.1 5.5 stack.2
  18.6 6.5 %all-to-all-start = ((bf16[4,512,2048]{1,2,0:T(8,128)(2,1)}), bf16[4,512,2048]{1,2,0:T(8,128)(2,1)}, u32[]{:S(2)}, u32[]{:S(2)}) async-start(bf16[4,512,2048]{1,2,0:T(8,128)(2,1)} %stack.2), calls=%async_computation | async-start | bytes 16777216 | tf_op jit(solution)/shard_map/all_to_all | solution.py:29
  25.1 1.8 multiply_cosine_fusion
  26.9 182.7 %all-to-all-done = bf16[4,512,2048]{1,2,0:T(8,128)(2,1)} async-done(((bf16[4,512,2048]{1,2,0:T(8,128)(2,1)}), bf16[4,512,2048]{1,2,0:T(8,128)(2,1)}, u32[]{:S(2)}, u32[]{:S(2)}) %all-to-all-start) | async-done | bytes 8388640 | tf_op jit(solution)/shard_map/all_to_all | solution.py:29
  209.5 5.2 multiply_reduce_fusion
  214.7 7.7 %fusion.21 = bf16[512,8192]{0,1:T(8,128)(2,1)} fusion(f32[8192]{0:T(1024)S(1)} %copy-done.8, f32[512]{0:T(512)S(1)} %add_rsqrt_fusion, bf16[4,512,2048]{1,2,0:T(8,128)(2,1)} %all-to-all-done), kind=kLoop, calls=%fused_computation.27 | loop fusion | flops 16777216 | bytes 16812032 | tf_op jit(solution)/shard_map/convert_element_type | solution.py:36
  222.5 19.4 %convolution_add_fusion = f32[512,1536]{1,0:T(8,128)S(1)} fusion(bf16[512,8192]{0,1:T(8,128)(2,1)} %fusion.21, bf16[8192,1536]{1,0:T(8,128)(2,1)} %all-gather.6.cloned.1.call-done, f32[1536]{0:T(1024)S(1)} %pad_maximum_fusion.3), kind=kOutput, calls=%fused_computation.31 | convolution fusion | flops 12885688320 | bytes 36706304 | tf_op jit(solution)/shard_map/dot_general | solution.py:39
  241.9 1.6 copy-done.2
  246.6 1.8 copy_bitcast_fusion
  249.1 9.0 %all-gather = s32[8,1,512]{2,1,0:T(1,128)S(1)} all-gather(s32[1,1,512]{2,1,0:T(1,128)S(1)} %bitcast.78), channel_id=1, replica_groups=mesh['seq'=8,'tensor'=4] {'seq'}, dimensions={0}, use_global_device_ids=true | all-gather | bytes 18432 | tf_op jit(solution)/shard_map/all_gather | solution.py:88
  261.8 11.9 %all-gather.8.cloned.1.call-done = bf16[4096,2,128]{2,0,1:T(8,128)(2,1)} async-done(((bf16[512,2,128]{2,0,1:T(8,128)(2,1)}), bf16[4096,2,128]{2,0,1:T(8,128)(2,1)}) %all-gather.8.cloned.1.call-update) | async-done | bytes 2097168 | tf_op jit(solution)/shard_map/all_gather | solution.py:86
  273.7 29.7 %all-gather.10.cloned.1.call-done = bf16[4096,2,128]{2,0,1:T(8,128)(2,1)} async-done(((bf16[512,2,128]{2,0,1:T(8,128)(2,1)}), bf16[4096,2,128]{2,0,1:T(8,128)(2,1)}) %all-gather.10.cloned.1.call-update) | async-done | bytes 2097168 | tf_op jit(solution)/shard_map/all_gather | solution.py:87
  303.4 97.0 %while.15 = (s32[]{:T(128)}, f32[2,4,512]{2,1,0:T(4,128)S(1)}, f32[2,4,512]{2,1,0:T(4,128)S(1)}, f32[2,4,512,128]{3,2,1,0:T(8,128)S(1)}, s32[2,2048]{1,0:T(2,128...) while((s32[]{:T(128)}, f32[2,4,512]{2,1,0:T(4,128)S(1)}, ...), condition=%wide.region_4.5_spmd.clone, body=%wide.region_1.4_spmd.clone.sunk | while | flops 4406661120 | bytes 112487544 | solution.py:100
  304.2 16.7 %fusion.41 = (f32[2,4,512]{2,1,0:T(4,128)S(1)}, f32[2,2048,512,4]{2,1,3,0:T(8,128)}) fusion(pred[512,2048]{0,1:T(8,128)(4,1)S(1)} %broadcast_compare_fusion.2, bf16[512,2,4,128]{3,0,2,1:T(8,128)(2,1)} %get-tuple-element.222, bf16[2,2048,2,128]{3,1,0,2:T(8,128)(2,1)} %get-tuple-element.221, s32[]{:T(128)} %get-tuple-element.204), kind=kOutput, calls=%fused_computation.2.clone.1 | convolution fusion | flops 2172645376 | bytes 36717056 | tf_op jit(solution)/shard_map/while/body/eval_jaxpr/tgcd,sgd->gcts/dot_general | solution.py:64
  320.9 14.9 %fusion.42 = f32[2,4,512]{2,1,0:T(4,128)S(1)} fusion(f32[2,2048,512,4]{2,1,3,0:T(8,128)} %get-tuple-element.190, f32[2,4,512]{2,1,0:T(4,128)S(1)} %select_maximum_fusion.2, pred[512,2048]{0,1:T(8,128)(4,1)S(1)} %broadcast_compare_fusion.2), kind=kLoop, calls=%fused_computation.4.clone.1 | loop fusion | flops 41938944 | bytes 34635776 | tf_op jit(solution)/shard_map/while/body/eval_jaxpr/reduce_sum | solution.py:72
  335.8 17.8 %fusion.44 = f32[2,4,512,128]{3,2,1,0:T(8,128)S(1)} fusion(f32[2,4,512,128]{3,2,1,0:T(8,128)S(1)} %get-tuple-element.207, f32[2,2048,512,4]{2,1,3,0:T(8,128)} %get-tuple-element.190, f32[2,4,512]{2,1,0:T(4,128)S(1)} %select_maximum_fusion.2, pred[512,2048]{0,1:T(8,128)(4,1)S(1)} %broadcast_compare_fusion.2, ...), kind=kOutput, calls=%fused_computation.8.clone.1 | convolution fusion | flops 2190999552 | bytes 39879168 | tf_op jit(solution)/shard_map/while/body/eval_jaxpr/gcts,sgd->gctd/dot_general | solution.py:73
  354.4 15.0 %fusion.41 = (f32[2,4,512]{2,1,0:T(4,128)S(1)}, f32[2,2048,512,4]{2,1,3,0:T(8,128)}) fusion(pred[512,2048]{0,1:T(8,128)(4,1)S(1)} %broadcast_compare_fusion.2, bf16[512,2,4,128]{3,0,2,1:T(8,128)(2,1)} %get-tuple-element.222, bf16[2,2048,2,128]{3,1,0,2:T(8,128)(2,1)} %get-tuple-element.221, s32[]{:T(128)} %get-tuple-element.204), kind=kOutput, calls=%fused_computation.2.clone.1 | convolution fusion | flops 2172645376 | bytes 36717056 | tf_op jit(solution)/shard_map/while/body/eval_jaxpr/tgcd,sgd->gcts/dot_general | solution.py:64
  369.5 15.4 %fusion.42 = f32[2,4,512]{2,1,0:T(4,128)S(1)} fusion(f32[2,2048,512,4]{2,1,3,0:T(8,128)} %get-tuple-element.190, f32[2,4,512]{2,1,0:T(4,128)S(1)} %select_maximum_fusion.2, pred[512,2048]{0,1:T(8,128)(4,1)S(1)} %broadcast_compare_fusion.2), kind=kLoop, calls=%fused_computation.4.clone.1 | loop fusion | flops 41938944 | bytes 34635776 | tf_op jit(solution)/shard_map/while/body/eval_jaxpr/reduce_sum | solution.py:72
  384.9 15.5 %fusion.44 = f32[2,4,512,128]{3,2,1,0:T(8,128)S(1)} fusion(f32[2,4,512,128]{3,2,1,0:T(8,128)S(1)} %get-tuple-element.207, f32[2,2048,512,4]{2,1,3,0:T(8,128)} %get-tuple-element.190, f32[2,4,512]{2,1,0:T(4,128)S(1)} %select_maximum_fusion.2, pred[512,2048]{0,1:T(8,128)(4,1)S(1)} %broadcast_compare_fusion.2, ...), kind=kOutput, calls=%fused_computation.8.clone.1 | convolution fusion | flops 2190999552 | bytes 39879168 | tf_op jit(solution)/shard_map/while/body/eval_jaxpr/gcts,sgd->gctd/dot_general | solution.py:73
  402.7 17.2 %convolution_convert_fusion = bf16[512,8192]{1,0:T(8,128)(2,1)} fusion(bf16[512,1024]{1,0:T(8,128)(2,1)S(1)} %convert_element_type.57, bf16[1024,8192]{1,0:T(8,128)(2,1)} %all-gather.12.cloned.1.call-done), kind=kOutput, calls=%fused_computation.29 | convolution fusion | flops 8594128896 | bytes 26214400 | tf_op jit(solution)/shard_map/dot_general | solution.py:108
  419.9 144.7 %reduce-scatter.2.cloned.1.call-done = bf16[512,2048]{1,0:T(8,128)(2,1)} async-done(((bf16[512,8192]{1,0:T(8,128)(2,1)}), bf16[512,2048]{1,0:T(8,128)(2,1)}) %reduce-scatter.2.cloned.1.call-update) | async-done | bytes 2097168 | tf_op jit(solution)/shard_map/reduce_scatter | solution.py:113
  564.6 3.7 add_convert_fusion
  (68 shorter events, 11.4 us)
Async XLA Ops:
  7.2 215.3 %all-gather.6.cloned.1.call-start = ((), (), s32[]{:S(2)}) async-start(), calls=%async_computation.2 | async-start | bytes 28311552 | tf_op jit(solution)/shard_map/all_gather | solution.py:40
  7.2 3.3 copy-start
  18.5 6.5 %copy-start.7 = (s32[512]{0:T(512)S(1)}, s32[512]{0:T(512)}, u32[]{:S(2)}) copy-start(s32[512]{0:T(512)} %param.13) | copy-start | bytes 6148
  18.5 6.5 %copy-start.9 = (f32[1024]{0:T(1024)S(1)}, f32[1024]{0:T(1024)}, u32[]{:S(2)}) copy-start(f32[1024]{0:T(1024)} %param.18) | copy-start | bytes 12292
  18.5 6.5 %copy-start.10 = (f32[256]{0:T(256)S(1)}, f32[256]{0:T(256)}, u32[]{:S(2)}) copy-start(f32[256]{0:T(256)} %param.20) | copy-start | bytes 3076
  18.6 6.5 %copy-start.11 = (f32[256]{0:T(256)S(1)}, f32[256]{0:T(256)}, u32[]{:S(2)}) copy-start(f32[256]{0:T(256)} %param.19) | copy-start | bytes 3076
  18.6 191.0 %all-to-all-start = ((bf16[4,512,2048]{1,2,0:T(8,128)(2,1)}), bf16[4,512,2048]{1,2,0:T(8,128)(2,1)}, u32[]{:S(2)}, u32[]{:S(2)}) async-start(bf16[4,512,2048]{1,2,0:T(8,128)(2,1)} %stack.2), calls=%async_computation | async-start | bytes 16777216 | tf_op jit(solution)/shard_map/all_to_all | solution.py:29
  25.0 248.6 %all-gather.8.cloned.1.call-start = ((), (), s32[]{:S(2)}) async-start(), calls=%async_computation.3 | async-start | bytes 2359296 | tf_op jit(solution)/shard_map/all_gather | solution.py:86
  26.9 187.8 %copy-start.8 = (f32[8192]{0:T(1024)S(1)}, f32[8192]{0:T(1024)}, u32[]{:S(2)}) copy-start(f32[8192]{0:T(1024)} %param.14) | copy-start | bytes 98308
  241.9 1.7 copy-start.2
  244.5 13.7 %copy-start.3 = (f32[512,1536]{1,0:T(8,128)S(1)}, f32[512,1536]{1,0:T(8,128)}, u32[]{:S(2)}) copy-start(f32[512,1536]{1,0:T(8,128)} %copy-done.2) | copy-start | bytes 9437188
  246.6 56.8 %all-gather.10.cloned.1.call-start = ((), (), s32[]{:S(2)}) async-start(), calls=%async_computation.4 | async-start | bytes 2359296 | tf_op jit(solution)/shard_map/all_gather | solution.py:87
  248.4 154.3 %all-gather.12.cloned.1.call-start = ((), (), s32[]{:S(2)}) async-start(), calls=%async_computation.5 | async-start | bytes 18874368 | tf_op jit(solution)/shard_map/all_gather | solution.py:110
  249.0 315.6 %reduce-scatter.2.cloned.1.call-start = ((), (), s32[]{:S(2)}) async-start(), calls=%async_computation.6 | async-start | bytes 10485760 | tf_op jit(solution)/shard_map/reduce_scatter | solution.py:113
  258.1 1.0 copy-start.4
  259.9 43.5 %copy-start.5 = (f32[2,4,512,128]{3,2,1,0:T(8,128)S(1)}, f32[2,4,512,128]{3,2,1,0:T(8,128)}, u32[]{:S(2)}) copy-start(f32[2,4,512,128]{3,2,1,0:T(8,128)} %custom-call.2) | copy-start | bytes 6291460
  402.7 17.2 %copy-start.6 = (bf16[512,1024]{1,0:T(8,128)(2,1)}, bf16[512,1024]{1,0:T(8,128)(2,1)S(1)}, u32[]{:S(2)}) copy-start(bf16[512,1024]{1,0:T(8,128)(2,1)S(1)} %convert_element_type.57) | copy-start | bytes 3145732
  419.9 144.7 %copy-start.1 = (bf16[512,2048]{1,0:T(8,128)(2,1)S(1)}, bf16[512,2048]{1,0:T(8,128)(2,1)}, u32[]{:S(2)}) copy-start(bf16[512,2048]{1,0:T(8,128)(2,1)} %param.12) | copy-start | bytes 6291460
Sparse Core Ops, SparseCore 0:
  10.7 127.9 all-gather.5
  246.7 26.9 all-gather.7
  275.6 27.7 all-gather.9
  305.2 89.7 all-gather.11
  420.1 144.5 reduce-scatter.1
